TPU v7x, 256 devices: a whole 4x4x8 slice. The times are simulated.
256 devices in a mesh: seq: 2 (over core), chan: 16 (over y, x), batch: 8 (over z).
Axes of the slice: x: 4, y: 4, z: 8, core: 2. Of those that a mesh axis runs over, the one named last changes fastest.
Arguments:
- ssm_input: bfloat16 [16384, 4096], P(('batch', 'seq'), 'chan'), parts along dimension 0, may hold values from -6 to 6
- gate_z: bfloat16 [16384, 4096], P(('batch', 'seq'), 'chan'), parts along dimension 0, may hold values from -6 to 6
- proj_forward: bfloat16 [2, 16384, 128], P(None, ('batch', 'seq')), parts along dimension 1, may hold values from -2 to 2
- proj_backward: bfloat16 [2, 16384, 128], P(None, ('batch', 'seq')), parts along dimension 1, may hold values from -2 to 2
- step_raw: float32 [2, 64, 16384], P(None, 'chan', ('batch', 'seq')), parts along dimension 2, may hold values from -3 to 3
- head_params: float32 [2, 2, 64], P(None, None, 'chan'), may hold values from -4 to 1, as said below
- skip_gain: float32 [64], P('chan'), may hold values from 0.25 to 2
- norm_gain: float32 [4096], P('chan'), may hold values from 0.5 to 1.5
- out_weight: bfloat16 [4096, 2048], P(None, 'chan'), may hold values from -0.09375 to 0.09375
Outputs:
- mixed: bfloat16 [16384, 2048], P(('batch', 'seq'), 'chan'), parts along dimension 0
There are 8 independent parts, one for each index of `batch`. A program takes and returns all parts, laid end to end along the dimension named above; an argument that names none is the same for every part. Nothing has to cross between parts.
Inputs may be any that keep to these rules, and one draw needn't show every extreme that they name: `head_params`: index 0 of the second dimension holds positive decay rates, index 1 time-step biases.
All inputs are finite; a program needn't handle non-finite values.
Results may differ from a plain program's by a relative error of at most 0.0085.
Values may be sent and summed in bfloat16 or wider, within the bound.
A program may use at most 128 MiB of HBM per device.

v0:
```python
import jax
import jax.numpy as jnp
from jax import lax
from jax.sharding import PartitionSpec as P

SPAN = 256
INNER = 4096


def sent_together(arrays, axis, dim, along):
    columns = [a.reshape(*a.shape[:along], -1) for a in arrays]
    both = jnp.concatenate(columns, axis=along)
    whole, at, done = (lax.all_gather(both, axis, axis=dim, tiled=True), 0, [])
    for a, column in zip(arrays, columns):
        slab = whole[..., at : at + column.shape[along]]
        done.append(slab.reshape(*slab.shape[:along], *a.shape[along:]))
        at += column.shape[along]
    return tuple(done)


def copy_for_each(value, axis):
    copies = jnp.broadcast_to(value, (lax.axis_size(axis), *value.shape))
    return lax.all_to_all(copies, axis, split_axis=0, concat_axis=0, tiled=True)


def taken_together(value, axis):
    everything = copy_for_each(value, axis)
    return jnp.sum(everything, axis=0)


def local_scan(blocks_x, b_rows, c_rows, steps_here, decay_rates):
    cumlog = jnp.cumsum(-decay_rates[None, :, None] * steps_here, axis=2)
    scores = jnp.einsum("cqn,csn->cqs", c_rows, b_rows, preferred_element_type=jnp.float32)
    lower_mask = jnp.tril(jnp.ones((SPAN, SPAN), dtype=bool))
    log_gaps = cumlog[:, :, :, None] - cumlog[:, :, None, :]
    decays = jnp.where(lower_mask, jnp.exp(jnp.where(lower_mask, log_gaps, 0.0)), 0.0)
    weights = (scores[:, None] * decays * steps_here[:, :, None, :]).astype(jnp.bfloat16)
    intra_out = jnp.einsum("chts,cshp->cthp", weights, blocks_x, preferred_element_type=jnp.float32)
    end_logs = cumlog[:, :, -1]
    in_weights = jnp.exp(end_logs[:, :, None] - cumlog) * steps_here
    b_weighted = (b_rows[:, None].astype(jnp.float32) * in_weights[..., None]).astype(jnp.bfloat16)
    block_states = jnp.einsum(
        "cshp,chsn->chpn", blocks_x, b_weighted, preferred_element_type=jnp.float32
    )

    def advance(carried, inputs):
        gain_log, block_state = inputs
        return (jnp.exp(gain_log)[:, None, None] * carried + block_state, carried)

    initial = jnp.zeros(block_states.shape[1:], jnp.float32)
    end_state, entering = lax.scan(advance, initial, (end_logs, block_states))
    before = jnp.cumsum(end_logs, axis=0) - end_logs
    whole_decay = jnp.exp(jnp.sum(end_logs, axis=0))
    return ((intra_out, entering, cumlog, before, c_rows), (whole_decay, end_state))


def finish(pieces, carried):
    intra_out, entering, cumlog, before, c_rows = pieces
    states = entering + jnp.exp(before)[:, :, None, None] * carried[None]
    inter = jnp.einsum("ctn,chpn->cthp", c_rows.astype(jnp.float32), states)
    inter = inter * jnp.exp(cumlog).transpose(0, 2, 1)[..., None]
    outputs = intra_out + inter
    return outputs.reshape(outputs.shape[0] * outputs.shape[1], -1)


def body(
    ssm_input,
    gate_z,
    proj_forward,
    proj_backward,
    step_raw,
    head_params,
    skip_gain,
    norm_gain,
    out_weight,
):
    frames, inner_here = ssm_input.shape
    heads_here = step_raw.shape[1]
    width = inner_here // heads_here
    blocks = frames // SPAN
    shape_x = (blocks, SPAN, heads_here, width)
    shape_rows = (blocks, SPAN, proj_forward.shape[2])

    def to_blocks(steps):
        return steps.reshape(heads_here, blocks, SPAN).transpose(1, 0, 2)

    steps_fwd = jax.nn.softplus(step_raw[0] + head_params[0, 1][:, None])
    steps_bwd = jax.nn.softplus(step_raw[1] + head_params[1, 1][:, None])[:, ::-1]
    fwd_parts, fwd_end = local_scan(
        ssm_input.reshape(shape_x),
        proj_forward[0].reshape(shape_rows),
        proj_forward[1].reshape(shape_rows),
        to_blocks(steps_fwd),
        head_params[0, 0],
    )
    bwd_parts, bwd_end = local_scan(
        ssm_input[::-1].reshape(shape_x),
        proj_backward[0][::-1].reshape(shape_rows),
        proj_backward[1][::-1].reshape(shape_rows),
        to_blocks(steps_bwd),
        head_params[1, 0],
    )
    decays_all, states_all = tuple(
        (
            part.astype(jnp.float32)
            for part in sent_together(
                (
                    jnp.stack([fwd_end[0], bwd_end[0]])[None].astype(jnp.bfloat16),
                    jnp.stack([fwd_end[1], bwd_end[1]])[None].astype(jnp.bfloat16),
                ),
                "seq",
                0,
                3,
            )
        )
    )
    own_index = lax.axis_index("seq")
    group_size = lax.axis_size("seq")

    def accumulate(position, carried):
        forward_state, backward_state = carried
        mirror = group_size - 1 - position
        forward_state = jnp.where(
            position < own_index,
            decays_all[position, 0][:, None, None] * forward_state + states_all[position, 0],
            forward_state,
        )
        backward_state = jnp.where(
            mirror > own_index,
            decays_all[mirror, 1][:, None, None] * backward_state + states_all[mirror, 1],
            backward_state,
        )
        return (forward_state, backward_state)

    empty_state = jnp.zeros(fwd_end[1].shape, jnp.float32)
    carry_fwd, carry_bwd = lax.fori_loop(0, group_size, accumulate, (empty_state, empty_state))
    forward_out = finish(fwd_parts, carry_fwd)
    backward_out = finish(bwd_parts, carry_bwd)[::-1]
    skipped = (
        ssm_input.reshape(frames, heads_here, width).astype(jnp.float32) * skip_gain[:, None]
    ).reshape(frames, inner_here)
    gated = (forward_out + backward_out + skipped) * jax.nn.silu(gate_z.astype(jnp.float32))
    squares = taken_together(jnp.sum(gated * gated, axis=1), "chan")
    scale = lax.rsqrt(squares / INNER + 1.0)
    normed = (gated * scale[:, None] * norm_gain).astype(jnp.bfloat16)
    frame_share = lax.all_to_all(normed, "chan", split_axis=0, concat_axis=1, tiled=True)
    projected = jnp.dot(
        frame_share,
        lax.all_gather(out_weight, "chan", axis=1, tiled=True),
        preferred_element_type=jnp.float32,
    ).astype(jnp.bfloat16)
    return lax.all_to_all(projected, "chan", split_axis=1, concat_axis=0, tiled=True)


def solution(mesh):
    in_specs = (
        P(("batch", "seq"), "chan"),
        P(("batch", "seq"), "chan"),
        P(None, ("batch", "seq"), None),
        P(None, ("batch", "seq"), None),
        P(None, "chan", ("batch", "seq")),
        P(None, None, "chan"),
        P("chan"),
        P("chan"),
        P(None, "chan"),
    )
    out_specs = P(("batch", "seq"), "chan")
    return jax.shard_map(body, mesh=mesh, in_specs=in_specs, out_specs=out_specs, check_vma=False)
```

profile of v0, /device:TPU:96, one launch (start us, length us, event | category | flops | bytes accessed | tf_op | source)
XLA Modules:
  0.0 171.4 jit_solution(11320585137728651989)
XLA Ops:
  7.3 1.2 copy.167
  8.5 6.3 %rev.17 = bf16[1024,256]{1,0:T(8,128)(2,1)S(1)} reverse(bf16[1024,256]{1,0:T(8,128)(2,1)} %param.15), dimensions={0} | reverse | bytes 1048576 | tf_op jit(solution)/shard_map/rev | solution.py:97
  16.4 0.8 compare_select_fusion
  18.0 4.8 %reduce-window.14 = f32[4,4,2,128]{3,2,1,0:T(2,128)S(1)} reduce-window(f32[4,4,2,128]{3,2,1,0:T(2,128)S(1)} %reshape.296, f32[]{:T(128)} %constant.83.clone.1), window={size=1x1x1x128 pad=0_0x0_0x0_0x127_0}, to_apply=%region_0.1 | reduce-window | flops 520192 | bytes 32772 | tf_op jit(solution)/shard_map/reduce-window
  23.6 1.1 fusion.56
  24.8 1.2 reshape.298
  26.6 1.9 %convolution_bitcast_fusion.3 = f32[4,4,64,128]{3,2,1,0:T(8,128)S(1)} fusion(f32[4,4,256]{2,1,0:T(4,128)S(1)} %get-tuple-element.329, f32[4,256,128]{2,1,0:T(8,128)S(1)} %convert_element_type.76, bf16[4,256,4,64]{1,0,3,2:T(4,128)(2,1)} %reshape.298), kind=kOutput, calls=%fused_computation.48 | convolution fusion | flops 68157440 | bytes 1589248 | tf_op jit(solution)/shard_map/cshp,chsn->chpn/dot_general | solution.py:42
  29.3 4.8 %reduce-window.16 = f32[4,4,2,128]{3,2,1,0:T(2,128)S(1)} reduce-window(f32[4,4,2,128]{3,2,1,0:T(2,128)S(1)} %reshape.300, f32[]{:T(128)} %constant.83.clone.1), window={size=1x1x1x128 pad=0_0x0_0x0_0x127_0}, to_apply=%region_6.7 | reduce-window | flops 520192 | bytes 32772 | tf_op jit(solution)/shard_map/reduce-window.2
  34.9 1.8 %slice_bitcast_fusion = (bf16[1024,128]{1,0:T(8,128)(2,1)}, bf16[1024,128]{1,0:T(8,128)(2,1)S(1)}) fusion(bf16[2,1024,128]{2,1,0:T(8,128)(2,1)} %param.18), kind=kLoop, calls=%fused_computation.70 | loop fusion | bytes 1048576 | tf_op jit(solution)/shard_map/squeeze | solution.py:99
  36.9 0.8 convert_element_type.78
  39.3 2.0 %convolution_bitcast_fusion.2 = f32[4,4,64,128]{3,2,1,0:T(8,128)S(1)} fusion(bf16[4,256,4,64]{1,3,2,0:T(8,128)(2,1)S(1)} %copy.176, f32[4,4,256]{2,1,0:T(4,128)S(1)} %get-tuple-element.324, f32[4,256,128]{2,1,0:T(8,128)} %convert_element_type.78), kind=kOutput, calls=%fused_computation.47 | convolution fusion | flops 68157440 | bytes 1589248 | tf_op jit(solution)/shard_map/cshp,chsn->chpn/dot_general | solution.py:42
  42.7 2.0 %all_gather.6 = bf16[2,2,4,8193]{3,2,1,0:T(4,128)(2,1)S(1)} all-gather(bf16[1,2,4,8193]{3,2,1,0:T(4,128)(2,1)S(1)} %maximum_maximum_fusion), channel_id=1, replica_groups=mesh['seq'=2,'chan'=16,'batch'=8] {'seq'}, dimensions={0}, use_global_device_ids=true | all-gather | bytes 393264 | tf_op jit(solution)/shard_map/all_gather | solution.py:13
  45.4 3.2 %rev.18 = bf16[1024,128]{1,0:T(8,128)(2,1)S(1)} reverse(bf16[1024,128]{1,0:T(8,128)(2,1)} %get-tuple-element.319), dimensions={0} | reverse | bytes 524288 | tf_op jit(solution)/shard_map/rev | solution.py:99
  49.6 3.1 %fusion.22 = f32[4,256,4,64]{1,3,2,0:T(8,128)} fusion(bf16[4,256,4,64]{1,3,2,0:T(8,128)(2,1)S(1)} %copy.176, f32[4,4,256]{2,1,0:T(4,128)} %bitcast.166, f32[4,4,256]{2,1,0:T(4,128)S(1)} %copy-done.9, f32[4,256,256]{2,1,0:T(8,128)S(1)} %fusion.58, pred[256,256]{1,0:T(8,128)(4,1)S(1)} %iota_compare_fusion), kind=kOutput, calls=%fused_computation.37 | convolution fusion | flops 140509184 | bytes 2719744 | tf_op jit(solution)/shard_map/chts,cshp->cthp/dot_general | solution.py:38
  53.8 1.6 fusion.25
  56.3 1.5 rev.19
  58.2 2.5 %fusion.23 = f32[4,256,4,64]{1,3,2,0:T(8,128)S(1)} fusion(f32[4,4,256]{2,1,0:T(4,128)S(1)} %copy-done.13, f32[4,4,256]{2,1,0:T(4,128)S(1)} %copy-done.7, f32[4,256,256]{2,1,0:T(8,128)S(1)} %fusion.57, pred[256,256]{1,0:T(8,128)(4,1)S(1)} %copy-done.11, bf16[4,256,4,64]{1,0,3,2:T(4,128)(2,1)} %reshape.298), kind=kOutput, calls=%fused_computation.38 | convolution fusion | flops 140509184 | bytes 2719744 | tf_op jit(solution)/shard_map/chts,cshp->cthp/dot_general | solution.py:38
  61.8 1.2 copy.198
  63.3 1.8 %multiply_reduce_fusion = (f32[1024]{0:T(1024)S(1)}, f32[1024,256]{0,1:T(8,128)S(1)}) fusion(bf16[1024,256]{0,1:T(8,128)(2,1)S(1)} %copy.182, f32[256]{0:T(256)S(1)} %mul.274, bf16[1024,256]{0,1:T(8,128)(2,1)S(1)} %copy.167, f32[1024,256]{0,1:T(8,128)} %bitcast.150, f32[1024,256]{0,1:T(8,128)S(1)} %rev.19), kind=kLoop, calls=%fused_computation.55 | loop fusion | flops 3144704 | bytes 4199424 | tf_op jit(solution)/shard_map/reduce_sum | solution.py:143
  65.2 15.2 %all_to_all.46 = f32[16,1,1024]{2,1,0:T(1,128)S(1)} all-to-all(f32[16,1,1024]{2,1,0:T(1,128)S(1)} %broadcast_in_dim.57), channel_id=1, replica_groups=mesh['seq'=2,'chan'=16,'batch'=8] {'chan'}, dimensions={0} | all-to-all | bytes 131072 | tf_op jit(solution)/shard_map/all_to_all | solution.py:23
  80.8 18.8 %all_to_all.44 = bf16[16,64,256]{2,1,0:T(8,128)(2,1)S(1)} all-to-all(bf16[16,64,256]{2,1,0:T(8,128)(2,1)S(1)} %bitcast.160), channel_id=1, replica_groups=mesh['seq'=2,'chan'=16,'batch'=8] {'chan'}, dimensions={0} | all-to-all | bytes 1048576 | tf_op jit(solution)/shard_map/all_to_all | solution.py:146
  99.7 42.4 %all-gather.2.cloned.1.call-done = bf16[4096,2048]{1,0:T(8,128)(2,1)} async-done(((bf16[4096,128]{1,0:T(8,128)(2,1)}), bf16[4096,2048]{1,0:T(8,128)(2,1)}) %all-gather.2.cloned.1.call-update) | async-done | bytes 16777232 | tf_op jit(solution)/shard_map/all_gather | solution.py:149
  142.1 8.8 %fusion.28 = bf16[8,16,8,128]{3,2,1,0:T(8,128)(2,1)S(1)} fusion(bf16[64,4096]{1,0:T(8,128)(2,1)S(1)} %bitcast.151, bf16[4096,2048]{1,0:T(8,128)(2,1)} %all-gather.2.cloned.1.call-done), kind=kOutput, calls=%fused_computation.49 | convolution fusion | flops 1073872896 | bytes 17563648 | tf_op jit(solution)/shard_map/dot_general | solution.py:147
  150.9 12.9 %all_to_all.45 = bf16[64,16,128]{2,0,1:T(8,128)(2,1)S(1)} all-to-all(bf16[64,16,128]{2,0,1:T(8,128)(2,1)S(1)} %bitcast.162), channel_id=1, replica_groups=mesh['seq'=2,'chan'=16,'batch'=8] {'chan'}, dimensions={1} | all-to-all | bytes 524288 | tf_op jit(solution)/shard_map/all_to_all | solution.py:152
  (143 shorter events, 16.7 us)
Async XLA Ops:
  6.5 135.5 %all-gather.2.cloned.1.call-start = ((), (), s32[]{:S(2)}) async-start(), calls=%async_computation.3 | async-start | bytes 17825792 | tf_op jit(solution)/shard_map/all_gather | solution.py:149
  17.9 20.8 %copy-start.5 = (f32[4,1024]{1,0:T(4,128)}, f32[4,1024]{1,0:T(4,128)S(1)}, u32[]{:S(2)}) copy-start(f32[4,1024]{1,0:T(4,128)S(1)} %rev.15) | copy-start | bytes 49156
  18.0 10.6 %copy-start.12 = (f32[4,4,256]{2,1,0:T(4,128)}, f32[4,4,256]{2,1,0:T(4,128)S(1)}, u32[]{:S(2)}) copy-start(f32[4,4,256]{2,1,0:T(4,128)S(1)} %get-tuple-element.314) | copy-start | bytes 49156
  23.3 3.3 %copy-start.6 = (f32[4,4,256]{2,1,0:T(4,128)}, f32[4,4,256]{2,1,0:T(4,128)S(1)}, u32[]{:S(2)}) copy-start(f32[4,4,256]{2,1,0:T(4,128)S(1)} %reduce_window_sum.59) | copy-start | bytes 49156
  29.2 7.5 %copy-start = (f32[4,4,64,128]{3,2,1,0:T(8,128)}, f32[4,4,64,128]{3,2,1,0:T(8,128)S(1)}, u32[]{:S(2)}) copy-start(f32[4,4,64,128]{3,2,1,0:T(8,128)S(1)} %get-tuple-element.216) | copy-start | bytes 1572868
  29.2 7.7 %copy-start.16 = (f32[4,4]{1,0:T(4,128)}, f32[4,4]{1,0:T(4,128)S(1)}, u32[]{:S(2)}) copy-start(f32[4,4]{1,0:T(4,128)S(1)} %get-tuple-element.516) | copy-start | bytes 196
  34.6 6.8 %copy-start.8 = (f32[4,4,256]{2,1,0:T(4,128)}, f32[4,4,256]{2,1,0:T(4,128)S(1)}, u32[]{:S(2)}) copy-start(f32[4,4,256]{2,1,0:T(4,128)S(1)} %reduce_window_sum.62) | copy-start | bytes 49156
  42.0 0.8 copy-start.2
  42.0 7.6 %copy-start.9 = (f32[4,4,256]{2,1,0:T(4,128)S(1)}, f32[4,4,256]{2,1,0:T(4,128)}, u32[]{:S(2)}) copy-start(f32[4,4,256]{2,1,0:T(4,128)} %copy-done.8) | copy-start | bytes 49156
  48.7 4.1 %copy-start.10 = (pred[256,256]{1,0:T(8,128)(4,1)}, pred[256,256]{1,0:T(8,128)(4,1)S(1)}, u32[]{:S(2)}) copy-start(pred[256,256]{1,0:T(8,128)(4,1)S(1)} %iota_compare_fusion) | copy-start | bytes 196612
  52.7 1.0 copy-start.3
  52.7 1.0 copy-start.15
  55.3 2.4 %copy-start.17 = (f32[4,4]{1,0:T(4,128)S(1)}, f32[4,4]{1,0:T(4,128)}, u32[]{:S(2)}) copy-start(f32[4,4]{1,0:T(4,128)} %copy-done.16) | copy-start | bytes 196
  55.3 2.8 %copy-start.7 = (f32[4,4,256]{2,1,0:T(4,128)S(1)}, f32[4,4,256]{2,1,0:T(4,128)}, u32[]{:S(2)}) copy-start(f32[4,4,256]{2,1,0:T(4,128)} %copy-done.6) | copy-start | bytes 49156
  55.4 2.8 %copy-start.11 = (pred[256,256]{1,0:T(8,128)(4,1)S(1)}, pred[256,256]{1,0:T(8,128)(4,1)}, u32[]{:S(2)}) copy-start(pred[256,256]{1,0:T(8,128)(4,1)} %copy-done.10) | copy-start | bytes 196612
  55.4 2.8 %copy-start.13 = (f32[4,4,256]{2,1,0:T(4,128)S(1)}, f32[4,4,256]{2,1,0:T(4,128)}, u32[]{:S(2)}) copy-start(f32[4,4,256]{2,1,0:T(4,128)} %copy-done.12) | copy-start | bytes 49156
  58.2 2.5 %copy-start.1 = (f32[4,4,64,128]{3,2,1,0:T(8,128)S(1)}, f32[4,4,64,128]{3,2,1,0:T(8,128)}, u32[]{:S(2)}) copy-start(f32[4,4,64,128]{3,2,1,0:T(8,128)} %copy-done) | copy-start | bytes 1572868
  58.2 2.5 %copy-start.14 = (f32[4,256,4]{1,2,0:T(4,128)S(1)}, f32[4,256,4]{1,2,0:T(4,128)}, u32[]{:S(2)}) copy-start(f32[4,256,4]{1,2,0:T(4,128)} %get-tuple-element.330) | copy-start | bytes 49156
  60.7 2.3 %copy-start.4 = (bf16[1024,256]{1,0:T(8,128)(2,1)S(1)}, bf16[1024,256]{1,0:T(8,128)(2,1)}, u32[]{:S(2)}) copy-start(bf16[1024,256]{1,0:T(8,128)(2,1)} %param.16) | copy-start | bytes 1572868
  60.7 2.5 %copy-start.19 = (f32[4]{0:T(128)S(1)}, f32[4]{0:T(128)}, u32[]{:S(2)}) copy-start(f32[4]{0:T(128)} %param.21) | copy-start | bytes 52
  61.8 18.7 %copy-start.18 = (f32[256]{0:T(256)S(1)}, f32[256]{0:T(256)}, u32[]{:S(2)}) copy-start(f32[256]{0:T(256)} %param.22) | copy-start | bytes 3076
Sparse Core Ops, SparseCore 0:
  9.7 132.2 all-gather.1
where the time goes:
time: 173 us; the launch traced here: 171 us
  blocking collectives  48.9 us (28%)
  waiting for transfers between devices  43.1 us (25%)
  local copies, waits for them, and re-layouts  26 us (15%)
  matrix products  20.8 us (12%)
  other arithmetic  18.2 us (11%)
  between operations  14 us (8%)
    all_gather x1, waiting for transfers between devices, body(): lax.all_gather(out_weight, 'chan', axis=1, tiled=True)  42.4 us
    all_to_all x1, blocking collectives, body(): lax.all_to_all(normed, 'chan', split_axis=0, concat_axis=1, tiled=True)  18.8 us
    all_to_all x1, blocking collectives, copy_for_each(): return lax.all_to_all(copies, axis, split_axis=0, concat_axis=0, tiled=True)  15.2 us
    all_to_all x1, blocking collectives, body(): lax.all_to_all(projected, 'chan', split_axis=1, concat_axis=0, tiled=True)  12.9 us
    another operation x8, other arithmetic  9.88 us
    dot_general x1, matrix products, body(): jnp.dot(frame_share, lax.all_gather(out_weight, 'chan', axis=1, tiled=Tru...  8.79 us
    rev x1, local copies, waits for them, and re-layouts, body(): ssm_input[::-1].reshape(shape_x)  6.33 us
    dot_general x2, matrix products, local_scan(): jnp.einsum('chts,cshp->cthp', weights, blocks_x, preferred_element_type=j...  5.62 us
  transfers between devices with their start and end apart: 1, of which 1 were waited for; matrix products, arithmetic and copies ran while one was open for 32% of the time, Pallas kernels for 0%

commit v1 on v0

--- a/solution.py
+++ b/solution.py
@@ -146,7 +146,9 @@
     frame_share = lax.all_to_all(normed, "chan", split_axis=0, concat_axis=1, tiled=True)
     projected = jnp.dot(
         frame_share,
-        lax.all_gather(out_weight, "chan", axis=1, tiled=True),
+        jnp.concatenate(
+            lax.all_to_all(jnp.stack([out_weight] * lax.axis_size("chan")), "chan", 0, 0), axis=1
+        ),
         preferred_element_type=jnp.float32,
     ).astype(jnp.bfloat16)
     return lax.all_to_all(projected, "chan", split_axis=1, concat_axis=0, tiled=True)

time: 173 us -> 360 us (2.08)
  waiting for transfers between devices: 43.1 us -> 252 us
  blocking collectives: 48.9 us -> 31.7 us
  between operations: 14 us -> 0.65 us
  starting transfers between devices: 0.01 us -> 8.89 us
  local copies, waits for them, and re-layouts: 26 us -> 30.7 us
    all_to_all x0 -> x2, waiting for transfers between devices: none -> 252 us  [the longest x1 243 us: body(): lax.all_to_all(jnp.stack([out_weight] * lax.axis_size('chan')), 'chan', 0...]
    all_gather x1 -> x0, waiting for transfers between devices: 42.4 us -> none  [body(): lax.all_gather(out_weight, 'chan', axis=1, tiled=True)]
    all_to_all x1 -> x0, blocking collectives: 18.8 us -> none  [body(): lax.all_to_all(normed, 'chan', split_axis=0, concat_axis=1, tiled=True)]
    all_to_all x0 -> x2, starting transfers between devices: none -> 8.89 us  [the longest x1 5.13 us: body(): lax.all_to_all(jnp.stack([out_weight] * lax.axis_size('chan')), 'chan', 0...]
    another operation x11 -> x12, local copies, waits for them, and re-layouts: 0.62 us -> 6.52 us  [the longest x1 5.91 us: body(): jnp.stack([out_weight] * lax.axis_size('chan'))]
  transfers between devices with their start and end apart: 1 -> 2, of which waited for: 1 -> 2; matrix products, arithmetic and copies ran while one was open for 32% -> 0% of each run, Pallas kernels for 0% -> 0%
where the time goes in v1:
time: 360 us; the launch traced here: 359 us
  waiting for transfers between devices  252 us (70%)
  blocking collectives  31.7 us (9%)
  local copies, waits for them, and re-layouts  30.7 us (9%)
  matrix products  19 us (5%)
  other arithmetic  15.7 us (4%)
  starting transfers between devices  8.89 us (2%)
    all_to_all x1, waiting for transfers between devices, body(): lax.all_to_all(jnp.stack([out_weight] * lax.axis_size('chan')), 'chan', 0...  243 us
    all_to_all x1, blocking collectives, body(): lax.all_to_all(projected, 'chan', split_axis=1, concat_axis=0, tiled=True)  15.2 us
    all_to_all x1, blocking collectives, copy_for_each(): return lax.all_to_all(copies, axis, split_axis=0, concat_axis=0, tiled=True)  14.5 us
    dot_general x1, matrix products, body(): jnp.dot(frame_share, jnp.concatenate(lax.all_to_all(jnp.stack([out_weight...  11 us
    another operation x8, other arithmetic  9.89 us
    all_to_all x1, waiting for transfers between devices, body(): lax.all_to_all(normed, 'chan', split_axis=0, concat_axis=1, tiled=True)  9.21 us
  transfers between devices with their start and end apart: 2, of which 2 were waited for; matrix products, arithmetic and copies ran while one was open for 0% of the time, Pallas kernels for 0%

profile of v1, /device:TPU:96, one launch (start us, length us, event | category | flops | bytes accessed | tf_op | source)
XLA Modules:
  0.0 359.0 jit_solution(18161798572122859605)
XLA Ops:
  0.1 1.3 copy.173
  1.4 6.3 %rev.17 = bf16[1024,256]{1,0:T(8,128)(2,1)S(1)} reverse(bf16[1024,256]{1,0:T(8,128)(2,1)} %param.15), dimensions={0} | reverse | bytes 1048576 | tf_op jit(solution)/shard_map/rev | solution.py:97
  9.2 0.8 compare_select_fusion
  10.9 4.8 %reduce-window.14 = f32[4,4,2,128]{3,2,1,0:T(2,128)S(1)} reduce-window(f32[4,4,2,128]{3,2,1,0:T(2,128)S(1)} %reshape.304, f32[]{:T(128)} %constant.83.clone.1), window={size=1x1x1x128 pad=0_0x0_0x0_0x127_0}, to_apply=%region_0.1 | reduce-window | flops 520192 | bytes 32772 | tf_op jit(solution)/shard_map/reduce-window
  16.5 4.8 %reduce-window.16 = f32[4,4,2,128]{3,2,1,0:T(2,128)S(1)} reduce-window(f32[4,4,2,128]{3,2,1,0:T(2,128)S(1)} %reshape.308, f32[]{:T(128)} %constant.83.clone.1), window={size=1x1x1x128 pad=0_0x0_0x0_0x127_0}, to_apply=%region_6.7 | reduce-window | flops 520192 | bytes 32772 | tf_op jit(solution)/shard_map/reduce-window.2
  22.4 1.2 reshape.306
  25.9 1.8 convolution_bitcast_fusion.3
  28.5 1.2 slice_bitcast_fusion
  30.1 1.0 convolution_bitcast_fusion.2
  31.9 2.0 all_gather.3
  35.6 2.1 copy.188
  38.9 1.4 fusion.22
  41.6 1.5 rev.19
  43.5 2.5 fusion.23
  48.0 14.5 %all_to_all.50 = f32[16,1,1024]{2,1,0:T(1,128)S(1)} all-to-all(f32[16,1,1024]{2,1,0:T(1,128)S(1)} %broadcast_in_dim.57), channel_id=1, replica_groups=mesh['seq'=2,'chan'=16,'batch'=8] {'chan'}, dimensions={0} | all-to-all | bytes 131072 | tf_op jit(solution)/shard_map/all_to_all | solution.py:23
  62.7 1.0 copy.190
  63.7 3.8 %all-to-all-start.1 = ((bf16[16,64,256]{2,1,0:T(8,128)(2,1)}), bf16[16,64,256]{2,1,0:T(8,128)(2,1)S(1)}, u32[]{:S(2)}, u32[]{:S(2)}) async-start(bf16[16,64,256]{2,1,0:T(8,128)(2,1)} %bitcast.34), calls=%async_computation.1 | async-start | bytes 1048576 | tf_op jit(solution)/shard_map/all_to_all | solution.py:146
  67.4 1.5 copy.192
  68.9 9.2 %all-to-all-done.1 = bf16[16,64,256]{2,1,0:T(8,128)(2,1)S(1)} async-done(((bf16[16,64,256]{2,1,0:T(8,128)(2,1)}), bf16[16,64,256]{2,1,0:T(8,128)(2,1)S(1)}, u32[]{:S(2)}, u32[]{:S(2)}) %all-to-all-start.1) | async-done | bytes 524320 | tf_op jit(solution)/shard_map/all_to_all | solution.py:146
  78.1 5.9 %stack.20 = bf16[16,4096,128]{1,2,0:T(8,128)(2,1)} broadcast(bf16[4096,128]{0,1:T(8,128)(2,1)S(1)} %copy.192), dimensions={1,2} | broadcast | bytes 17825792 | tf_op jit(solution)/shard_map/stack | solution.py:150
  84.0 5.1 %all-to-all-start.2 = ((bf16[16,4096,128]{1,2,0:T(8,128)(2,1)}), bf16[16,4096,128]{1,2,0:T(8,128)(2,1)}, u32[]{:S(2)}, u32[]{:S(2)}) async-start(bf16[16,4096,128]{1,2,0:T(8,128)(2,1)} %stack.20), calls=%async_computation.2 | async-start | bytes 33554432 | tf_op jit(solution)/shard_map/all_to_all | solution.py:150
  89.2 242.9 %all-to-all-done.2 = bf16[16,4096,128]{1,2,0:T(8,128)(2,1)} async-done(((bf16[16,4096,128]{1,2,0:T(8,128)(2,1)}), bf16[16,4096,128]{1,2,0:T(8,128)(2,1)}, u32[]{:S(2)}, u32[]{:S(2)}) %all-to-all-start.2) | async-done | bytes 16777248 | tf_op jit(solution)/shard_map/all_to_all | solution.py:150
  332.1 11.0 %fusion.28 = bf16[8,16,8,128]{3,2,1,0:T(8,128)(2,1)S(1)} fusion(bf16[64,4096]{1,0:T(8,128)(2,1)S(1)} %bitcast.162, bf16[4096,2048]{0,1:T(8,128)(2,1)} %bitcast.37), kind=kOutput, calls=%fused_computation.49 | convolution fusion | flops 1073872896 | bytes 17563648 | tf_op jit(solution)/shard_map/dot_general | solution.py:147
  343.1 15.2 %all_to_all.49 = bf16[64,16,128]{2,0,1:T(8,128)(2,1)S(1)} all-to-all(bf16[64,16,128]{2,0,1:T(8,128)(2,1)S(1)} %bitcast.164), channel_id=1, replica_groups=mesh['seq'=2,'chan'=16,'batch'=8] {'chan'}, dimensions={1} | all-to-all | bytes 524288 | tf_op jit(solution)/shard_map/all_to_all | solution.py:154
  (141 shorter events, 16.7 us)
Async XLA Ops:
  0.0 24.5 %copy-start.8 = (bf16[2,1024,128]{2,1,0:T(8,128)(2,1)S(1)}, bf16[2,1024,128]{2,1,0:T(8,128)(2,1)}, u32[]{:S(2)}) copy-start(bf16[2,1024,128]{2,1,0:T(8,128)(2,1)} %param.17) | copy-start | bytes 1572868
  0.0 38.9 %copy-start.9 = (pred[256,256]{1,0:T(8,128)(4,1)}, pred[256,256]{1,0:T(8,128)(4,1)S(1)}, u32[]{:S(2)}) copy-start(pred[256,256]{1,0:T(8,128)(4,1)S(1)} %iota_compare_fusion) | copy-start | bytes 196612
  10.9 17.0 %copy-start.11 = (f32[4,4,256]{2,1,0:T(4,128)}, f32[4,4,256]{2,1,0:T(4,128)S(1)}, u32[]{:S(2)}) copy-start(f32[4,4,256]{2,1,0:T(4,128)S(1)} %get-tuple-element.314) | copy-start | bytes 49156
  25.2 4.8 %copy-start = (bf16[1,1024,128]{2,1,0:T(8,128)(2,1)}, bf16[1,1024,128]{2,1,0:T(8,128)(2,1)S(1)}, u32[]{:S(2)}) copy-start(bf16[1,1024,128]{2,1,0:T(8,128)(2,1)S(1)} %get-tuple-element.321) | copy-start | bytes 786436
  28.4 1.6 copy-start.3
  30.0 4.3 %copy-start.17 = (f32[4]{0:T(128)S(1)}, f32[4]{0:T(128)}, u32[]{:S(2)}) copy-start(f32[4]{0:T(128)} %param.21) | copy-start | bytes 52
  31.7 2.2 copy-start.5
  38.9 1.4 copy-start.6
  40.3 2.8 copy-start.1
  40.3 2.8 copy-start.2
  40.7 2.7 copy-start.10
  40.7 2.7 copy-start.12
  43.5 2.6 copy-start.4
  43.5 2.6 copy-start.13
  43.5 2.6 copy-start.14
  46.0 1.3 copy-start.7
  46.0 1.3 copy-start.15
  46.4 16.1 %copy-start.16 = (f32[256]{0:T(256)S(1)}, f32[256]{0:T(256)}, u32[]{:S(2)}) copy-start(f32[256]{0:T(256)} %param.22) | copy-start | bytes 3076
  63.7 14.5 %all-to-all-start.1 = ((bf16[16,64,256]{2,1,0:T(8,128)(2,1)}), bf16[16,64,256]{2,1,0:T(8,128)(2,1)S(1)}, u32[]{:S(2)}, u32[]{:S(2)}) async-start(bf16[16,64,256]{2,1,0:T(8,128)(2,1)} %bitcast.34), calls=%async_computation.1 | async-start | bytes 1048576 | tf_op jit(solution)/shard_map/all_to_all | solution.py:146
  84.0 248.1 %all-to-all-start.2 = ((bf16[16,4096,128]{1,2,0:T(8,128)(2,1)}), bf16[16,4096,128]{1,2,0:T(8,128)(2,1)}, u32[]{:S(2)}, u32[]{:S(2)}) async-start(bf16[16,4096,128]{1,2,0:T(8,128)(2,1)} %stack.20), calls=%async_computation.2 | async-start | bytes 33554432 | tf_op jit(solution)/shard_map/all_to_all | solution.py:150
